TPU v7x, 32 devices: a whole 2x2x4 slice. The times are simulated.
32 devices in a mesh: row: 8 (over y, x, core), col: 4 (over z).
Axes of the slice: x: 2, y: 2, z: 4, core: 2. Of those that a mesh axis runs over, the one named last changes fastest.
Arguments:
- queries: bfloat16 [8, 128, 4096], P(None, 'row', 'col'), may hold values from -13 to 13, as said below
- key_cache: bfloat16 [8, 16384, 1024], P(None, ('row', 'col')), may hold values from -13 to 13
- value_cache: bfloat16 [8, 16384, 1024], P(None, ('row', 'col')), may hold values from -6 to 6
- key_table: bfloat16 [1024, 1024], replicated, may hold values from -24 to 24
- value_table: bfloat16 [1024, 1024], replicated, may hold values from -6 to 6
- lengths: int32 [8], replicated, may hold values from 2048 to 16384
- token_ids: int32 [8, 128], P(None, 'row'), may hold values from 0 to 1023
Outputs:
- attended: bfloat16 [8, 128, 4096], P(None, 'row', 'col')
Inputs may be any that keep to these rules, and one draw needn't show every extreme that they name: `queries`: entries of the query array lie in the stated range.
All inputs are finite; a program needn't handle non-finite values.
Results may differ from a plain program's by a relative error of at most 0.006.
Values may be sent and summed in bfloat16 or wider, within the bound.
A program may use at most 192 MiB of HBM per device.

v0:
```python
import jax
import jax.numpy as jnp
from jax import lax
from jax.sharding import PartitionSpec as P

HQ = 32
KH = 8
HD = 128


def cache_partials(whole, key_cache, value_cache, lengths, offset):
    users, beams, width = whole.shape
    positions = key_cache.shape[1]
    group = HQ // KH
    scale = HD ** (-0.5)

    def one_user(items):
        q_user, k_user, v_user, limit = items
        q_heads = q_user.reshape(beams, KH, group, HD)
        k_heads = k_user.reshape(positions, KH, HD)
        v_heads = v_user.reshape(positions, KH, HD)
        s = (
            jnp.einsum("wkgd,lkd->kwgl", q_heads, k_heads, preferred_element_type=jnp.float32)
            * scale
        )
        live = offset + jnp.arange(positions, dtype=jnp.int32) < limit
        s = jnp.where(live, s, -1e30)
        peak = jnp.max(s, axis=-1)
        weight = jnp.where(live, jnp.exp(s - peak[..., None]), 0.0)
        total = jnp.sum(weight, axis=-1)
        numer = jnp.einsum(
            "kwgl,lkd->wkgd",
            weight.astype(jnp.bfloat16),
            v_heads,
            preferred_element_type=jnp.float32,
        )
        peak = jnp.transpose(peak, (1, 0, 2)).reshape(beams, HQ)
        total = jnp.transpose(total, (1, 0, 2)).reshape(beams, HQ)
        return (numer.reshape(beams, width), peak, total)

    return lax.map(one_user, (whole, key_cache, value_cache, lengths))


def body(queries, key_cache, value_cache, key_table, value_table, lengths, token_ids):
    users, beam_part, width_part = queries.shape
    heads_part = width_part // HD
    scale = HD ** (-0.5)
    row_at = lax.axis_index("row")
    col_at = lax.axis_index("col")
    whole = lax.all_gather(queries, "col", axis=2, tiled=True)
    whole = lax.all_gather(whole, "row", axis=1, tiled=True)
    offset = (row_at * lax.axis_size("col") + col_at) * key_cache.shape[1]
    numer_part, peak_part, total_part = cache_partials(
        whole, key_cache, value_cache, lengths, offset
    )
    peak_all = lax.pmax(peak_part, ("row", "col"))
    factor = jnp.exp(peak_part - peak_all)
    weighted = (numer_part.reshape(users, -1, HQ, HD) * factor[..., None]).reshape(
        users, -1, HQ * HD
    )
    mass = total_part * factor

    def local_part(array, per_head):
        picked = lax.dynamic_slice_in_dim(array, row_at * beam_part, beam_part, 1)
        return lax.dynamic_slice_in_dim(
            picked, col_at * heads_part * per_head, heads_part * per_head, 2
        )

    numer, total = lax.psum((weighted, mass), ("row", "col"))
    numer = local_part(numer, HD)
    total = local_part(total, 1)
    peak = local_part(peak_all, 1)
    codes = jnp.arange(key_table.shape[0], dtype=jnp.int32)
    onehot = (token_ids[..., None] == codes).astype(jnp.bfloat16)
    own_keys = jnp.einsum("uwv,vc->uwc", onehot, key_table, preferred_element_type=jnp.float32)
    own_values = jnp.einsum("uwv,vc->uwc", onehot, value_table, preferred_element_type=jnp.float32)
    group = HQ // KH
    own_keys = jnp.repeat(own_keys.reshape(users, beam_part, KH, HD), group, axis=2)
    own_values = jnp.repeat(own_values.reshape(users, beam_part, KH, HD), group, axis=2)
    own_keys = lax.dynamic_slice_in_dim(own_keys, col_at * heads_part, heads_part, 2)
    own_values = lax.dynamic_slice_in_dim(own_values, col_at * heads_part, heads_part, 2)
    q_local = queries.astype(jnp.float32).reshape(users, beam_part, heads_part, HD)
    own_score = jnp.sum(q_local * own_keys, axis=-1) * scale
    final_peak = jnp.maximum(peak, own_score)
    carried = jnp.exp(peak - final_peak)
    fresh = jnp.exp(own_score - final_peak)
    numer = (
        numer.reshape(users, beam_part, heads_part, HD) * carried[..., None]
        + fresh[..., None] * own_values
    )
    total = total * carried + fresh
    result = numer / total[..., None]
    return result.reshape(users, beam_part, width_part).astype(jnp.bfloat16)


def solution(mesh):
    return jax.shard_map(
        body,
        mesh=mesh,
        in_specs=(
            P(None, "row", "col"),
            P(None, ("row", "col"), None),
            P(None, ("row", "col"), None),
            P(),
            P(),
            P(),
            P(None, "row"),
        ),
        out_specs=P(None, "row", "col"),
        check_vma=False,
    )
```

profile of v0, /device:TPU:0, one launch (start us, length us, event | category | flops | bytes accessed | tf_op | source)
XLA Modules:
  0.0 730.9 jit_solution(4568035272929321944)
XLA Ops:
  6.5 1.9 copy.35
  8.6 31.1 %all-gather.3.cloned.1.call-done = bf16[8,16,4096]{2,0,1:T(8,128)(2,1)} async-done(((bf16[8,16,1024]{2,0,1:T(8,128)(2,1)}), bf16[8,16,4096]{2,0,1:T(8,128)(2,1)}) %all-gather.3.cloned.1.call-update) | async-done | bytes 1048592 | tf_op jit(solution)/shard_map/all_gather | solution.py:50
  39.8 55.4 %all-gather.5.cloned.1.call-done = bf16[8,128,4096]{2,0,1:T(8,128)(2,1)} async-done(((bf16[8,16,4096]{2,0,1:T(8,128)(2,1)}), bf16[8,128,4096]{2,0,1:T(8,128)(2,1)}) %all-gather.5.cloned.1.call-update) | async-done | bytes 8388624 | tf_op jit(solution)/shard_map/all_gather | solution.py:51
  95.2 12.5 %copy.37 = bf16[8,128,4096]{1,2,0:T(8,128)(2,1)} copy(bf16[8,128,4096]{2,0,1:T(8,128)(2,1)} %all-gather.5.cloned.1.call-done) | data formatting | bytes 16777216 | tf_op jit(solution)/shard_map/while | solution.py:41
  107.7 186.9 %while.14 = (s32[]{:T(128)}, f32[8,128,4096]{1,2,0:T(8,128)}, f32[8,128,32]{1,2,0:T(8,128)}, f32[8,128,32]{1,2,0:T(8,128)S(1)}, bf16[8,512,1024]{2,1,0:T(8,128)(...) while((s32[]{:T(128)}, f32[8,128,4096]{1,2,0:T(8,128)}, ...), condition=%wide.region_3.4_spmd, body=%wide.region_0.3_spmd.sunk | while | flops 1100997632 | bytes 78777504 | solution.py:41
  110.3 1.4 copy.58
  112.9 2.8 fusion.35
  115.8 3.2 copy-done.1
  119.0 2.3 fusion.37
  123.3 1.4 copy.57
  124.6 5.0 fusion.36
  129.6 1.5 constant_dynamic-update-slice_fusion.2
  133.6 1.4 copy.58
  136.3 2.8 fusion.35
  139.1 3.2 copy-done.1
  142.4 2.3 fusion.37
  146.6 1.4 copy.57
  148.0 5.0 fusion.36
  152.9 1.5 constant_dynamic-update-slice_fusion.2
  157.0 1.4 copy.58
  159.6 2.8 fusion.35
  162.5 3.2 copy-done.1
  165.7 2.3 fusion.37
  170.0 1.4 copy.57
  171.3 5.0 fusion.36
  176.3 1.5 constant_dynamic-update-slice_fusion.2
  180.3 1.4 copy.58
  183.0 2.8 fusion.35
  185.8 3.2 copy-done.1
  189.1 2.3 fusion.37
  193.3 1.4 copy.57
  194.7 5.0 fusion.36
  199.6 1.5 constant_dynamic-update-slice_fusion.2
  203.7 1.4 copy.58
  206.4 2.8 fusion.35
  209.2 3.2 copy-done.1
  212.4 2.3 fusion.37
  218.1 5.0 fusion.36
  223.0 1.5 constant_dynamic-update-slice_fusion.2
  227.1 1.4 copy.58
  229.7 2.8 fusion.35
  232.6 3.2 copy-done.1
  235.8 2.3 fusion.37
  241.4 5.0 fusion.36
  246.4 1.5 constant_dynamic-update-slice_fusion.2
  250.5 1.4 copy.58
  253.1 2.8 fusion.35
  256.0 3.2 copy-done.1
  259.2 2.3 fusion.37
  264.8 5.0 fusion.36
  269.8 1.5 constant_dynamic-update-slice_fusion.2
  273.8 1.4 copy.58
  276.5 2.8 fusion.35
  279.3 3.2 copy-done.1
  282.6 2.3 fusion.37
  288.2 5.0 fusion.36
  293.1 1.4 constant_dynamic-update-slice_fusion.2
  294.7 124.8 %all-reduce.4.cloned.1.call-done = f32[8,128,32]{1,2,0:T(8,128)} async-done(((f32[8,128,32]{1,2,0:T(8,128)}), f32[8,128,32]{1,2,0:T(8,128)}) %all-reduce.4.cloned.1.call-update) | async-done | bytes 131088 | tf_op jit(solution)/shard_map/pmax | solution.py:56
  419.4 1.7 fusion.20
  421.1 11.3 %bitcast_multiply_fusion = f32[8,128,4096]{1,2,0:T(8,128)} fusion(f32[8,128,4096]{1,2,0:T(8,128)} %get-tuple-element.54, f32[8,128,32]{1,2,0:T(8,128)S(1)} %get-tuple-element.117), kind=kLoop, calls=%fused_computation.17 | loop fusion | flops 4194304 | bytes 33685504 | tf_op jit(solution)/shard_map/mul | solution.py:58
  434.6 2.1 fusion.9
  436.8 276.3 %all-reduce.6.cloned.1.call-done = (f32[8,128,4096]{1,2,0:T(8,128)}, f32[8,128,32]{1,2,0:T(8,128)}) async-done(((f32[8,128,4096]{1,2,0:T(8,128)}, f32[8,128,32]{1,2,0:T(8,128)}), (f32[8,128,4096]{1,2,0:T(8,128)}, f32[8,128,32]{1,2,0:T(8,128)})) %all-reduce.6.cloned.1.call-update) | async-done | bytes 16908304 | tf_op jit(solution)/shard_map/psum | solution.py:69
  714.4 5.3 constant_dynamic-slice_fusion.3
  719.7 2.8 copy.49
  (93 shorter events, 57.1 us)
Async XLA Ops:
  6.5 425.9 %copy-start = (bf16[1024,1024]{1,0:T(8,128)(2,1)S(1)}, bf16[1024,1024]{1,0:T(8,128)(2,1)}, u32[]{:S(2)}) copy-start(bf16[1024,1024]{1,0:T(8,128)(2,1)} %param.12) | copy-start | bytes 6291460
  6.5 33.1 %all-gather.3.cloned.1.call-start = ((), (), s32[]{:S(2)}) async-start(), calls=%async_computation | async-start | bytes 1310720 | tf_op jit(solution)/shard_map/all_gather | solution.py:50
  8.5 86.7 %all-gather.5.cloned.1.call-start = ((), (), s32[]{:S(2)}) async-start(), calls=%async_computation.1 | async-start | bytes 9437184 | tf_op jit(solution)/shard_map/all_gather | solution.py:51
  39.7 379.7 %all-reduce.4.cloned.1.call-start = ((), (), s32[]{:S(2)}) async-start(), calls=%async_computation.2 | async-start | bytes 262144 | tf_op jit(solution)/shard_map/pmax | solution.py:56
  39.8 67.9 %copy-start.4 = (s32[8]{0:T(128)S(1)}, s32[8]{0:T(128)}, u32[]{:S(2)}) copy-start(s32[8]{0:T(128)} %param.14) | copy-start | bytes 100
  115.8 3.2 copy-start.1
  139.1 3.2 copy-start.1
  162.5 3.2 copy-start.1
  185.8 3.2 copy-start.1
  209.2 3.2 copy-start.1
  232.6 3.2 copy-start.1
  256.0 3.2 copy-start.1
  279.3 3.2 copy-start.1
  294.6 418.6 %all-reduce.6.cloned.1.call-start = ((), (), s32[]{:S(2)}) async-start(), calls=%async_computation.3 | async-start | bytes 33816576 | tf_op jit(solution)/shard_map/psum | solution.py:69
  432.4 0.7 copy-start.3
  432.4 1.3 copy-start.2
Sparse Core Ops, SparseCore 0:
  8.9 30.6 all-gather.2
  41.5 53.6 all-gather.4
  294.7 124.6 all-reduce.3
  432.5 280.6 all-reduce.5
where the time goes:
time: 733 us; the launch traced here: 731 us
  waiting for transfers between devices  488 us (67%)
  local copies, waits for them, and re-layouts  126 us (17%)
  matrix products  65 us (9%)
  other arithmetic  38.3 us (5%)
  between operations  13.3 us (2%)
    psum x1, waiting for transfers between devices, body(): numer, total = lax.psum((weighted, mass), ('row', 'col'))  276 us
    pmax x1, waiting for transfers between devices, body(): peak_all = lax.pmax(peak_part, ('row', 'col'))  125 us
    dynamic_slice x48, local copies, waits for them, and re-layouts, cache_partials(): return lax.map(one_user, (whole, key_cache, value_cache, lengths))  57.9 us
    all_gather x1, waiting for transfers between devices, body(): whole = lax.all_gather(whole, 'row', axis=1, tiled=True)  55.4 us
    dot_general x8, matrix products, one_user(): jnp.einsum('kwgl,lkd->wkgd', weight.astype(jnp.bfloat16), v_heads, prefer...  39.7 us
    all_gather x1, waiting for transfers between devices, body(): whole = lax.all_gather(queries, 'col', axis=2, tiled=True)  31.1 us
    while x16, local copies, waits for them, and re-layouts  25.8 us
    dot_general x8, matrix products, one_user(): jnp.einsum('wkgd,lkd->kwgl', q_heads, k_heads, preferred_element_type=jnp...  22.7 us
  transfers between devices with their start and end apart: 4, of which 4 were waited for; matrix products, arithmetic and copies ran while one was open for 1% of the time, Pallas kernels for 0%

commit v1 on v0

--- a/solution.py
+++ b/solution.py
@@ -66,7 +66,7 @@
             picked, col_at * heads_part * per_head, heads_part * per_head, 2
         )
 
-    numer, total = lax.psum((weighted, mass), ("row", "col"))
+    numer, total = lax.psum(lax.psum((weighted, mass), "col"), "row")
     numer = local_part(numer, HD)
     total = local_part(total, 1)
     peak = local_part(peak_all, 1)

time: 733 us -> 1240 us (1.69)
  waiting for transfers between devices: 488 us -> 993 us
    psum x1 -> x2, waiting for transfers between devices: 276 us -> 782 us  [body(): numer, total = lax.psum(lax.psum((weighted, mass), 'col'), 'row')]
  transfers between devices with their start and end apart: 4 -> 5, of which waited for: 4 -> 5; matrix products, arithmetic and copies ran while one was open for 1% -> 0% of each run, Pallas kernels for 0% -> 0%
where the time goes in v1:
time: 1240 us
  waiting for transfers between devices  993 us (80%)
  local copies, waits for them, and re-layouts  126 us (10%)
  matrix products  65 us (5%)
  other arithmetic  38.9 us (3%)
  between operations  13.3 us (1%)
    psum x2, waiting for transfers between devices, body(): numer, total = lax.psum(lax.psum((weighted, mass), 'col'), 'row')  782 us
    pmax x1, waiting for transfers between devices, body(): peak_all = lax.pmax(peak_part, ('row', 'col'))  125 us
    dynamic_slice x48, local copies, waits for them, and re-layouts, cache_partials(): return lax.map(one_user, (whole, key_cache, value_cache, lengths))  58.2 us
    all_gather x1, waiting for transfers between devices, body(): whole = lax.all_gather(whole, 'row', axis=1, tiled=True)  55.4 us
    dot_general x8, matrix products, one_user(): jnp.einsum('kwgl,lkd->wkgd', weight.astype(jnp.bfloat16), v_heads, prefer...  39.7 us
    all_gather x1, waiting for transfers between devices, body(): whole = lax.all_gather(queries, 'col', axis=2, tiled=True)  31.1 us
    while x16, local copies, waits for them, and re-layouts  25.7 us
  transfers between devices with their start and end apart: 5, of which 5 were waited for; matrix products, arithmetic and copies ran while one was open for 0% of the time, Pallas kernels for 0%

profile of v1, /device:TPU:0, one launch (start us, length us, event | category | flops | bytes accessed | tf_op | source)
XLA Modules:
  0.0 1237.1 jit_solution(2894487895881263465)
XLA Ops:
  6.5 1.9 copy.35
  8.6 31.1 %all-gather.3.cloned.1.call-done = bf16[8,16,4096]{2,0,1:T(8,128)(2,1)} async-done(((bf16[8,16,1024]{2,0,1:T(8,128)(2,1)}), bf16[8,16,4096]{2,0,1:T(8,128)(2,1)}) %all-gather.3.cloned.1.call-update) | async-done | bytes 1048592 | tf_op jit(solution)/shard_map/all_gather | solution.py:50
  39.8 55.4 %all-gather.5.cloned.1.call-done = bf16[8,128,4096]{2,0,1:T(8,128)(2,1)} async-done(((bf16[8,16,4096]{2,0,1:T(8,128)(2,1)}), bf16[8,128,4096]{2,0,1:T(8,128)(2,1)}) %all-gather.5.cloned.1.call-update) | async-done | bytes 8388624 | tf_op jit(solution)/shard_map/all_gather | solution.py:51
  95.2 12.5 %copy.37 = bf16[8,128,4096]{1,2,0:T(8,128)(2,1)} copy(bf16[8,128,4096]{2,0,1:T(8,128)(2,1)} %all-gather.5.cloned.1.call-done) | data formatting | bytes 16777216 | tf_op jit(solution)/shard_map/while | solution.py:41
  107.7 187.6 %while.14 = (s32[]{:T(128)}, f32[8,128,4096]{1,2,0:T(8,128)}, f32[8,128,32]{1,2,0:T(8,128)}, f32[8,128,32]{1,2,0:T(8,128)S(1)}, bf16[8,512,1024]{2,1,0:T(8,128)(...) while((s32[]{:T(128)}, f32[8,128,4096]{1,2,0:T(8,128)}, ...), condition=%wide.region_3.4_spmd, body=%wide.region_0.3_spmd.sunk | while | flops 1100997632 | bytes 78777504 | solution.py:41
  110.3 1.4 copy.58
  113.0 2.8 fusion.35
  115.9 3.2 copy-done.1
  119.1 2.3 fusion.37
  123.3 1.4 copy.57
  124.7 5.0 fusion.36
  129.7 1.5 constant_dynamic-update-slice_fusion.2
  133.8 1.4 copy.58
  136.5 2.8 fusion.35
  139.3 3.2 copy-done.1
  142.5 2.3 fusion.37
  148.1 5.0 fusion.36
  153.1 1.5 constant_dynamic-update-slice_fusion.2
  157.2 1.4 copy.58
  159.9 2.8 fusion.35
  162.7 3.2 copy-done.1
  166.0 2.3 fusion.37
  171.6 5.0 fusion.36
  176.5 1.5 constant_dynamic-update-slice_fusion.2
  180.7 1.4 copy.58
  183.3 2.8 fusion.35
  186.2 3.2 copy-done.1
  189.4 2.3 fusion.37
  193.7 1.4 copy.57
  195.0 5.0 fusion.36
  200.0 1.5 constant_dynamic-update-slice_fusion.2
  204.1 1.4 copy.58
  206.8 2.8 fusion.35
  209.6 3.2 copy-done.1
  212.9 2.3 fusion.37
  218.5 5.0 fusion.36
  223.4 1.5 constant_dynamic-update-slice_fusion.2
  227.6 1.4 copy.58
  230.3 2.8 fusion.35
  233.1 3.2 copy-done.1
  236.4 2.3 fusion.37
  240.6 1.4 copy.57
  242.0 5.0 fusion.36
  246.9 1.5 constant_dynamic-update-slice_fusion.2
  251.1 1.4 copy.58
  253.7 2.8 fusion.35
  256.6 3.2 copy-done.1
  259.8 2.3 fusion.37
  265.4 5.0 fusion.36
  270.4 1.5 constant_dynamic-update-slice_fusion.2
  274.5 1.4 copy.58
  277.2 2.8 fusion.35
  280.0 3.2 copy-done.1
  283.2 2.3 fusion.37
  288.8 5.0 fusion.36
  293.8 1.4 constant_dynamic-update-slice_fusion.2
  295.3 124.8 %all-reduce.6.cloned.1.call-done = f32[8,128,32]{1,2,0:T(8,128)} async-done(((f32[8,128,32]{1,2,0:T(8,128)}), f32[8,128,32]{1,2,0:T(8,128)}) %all-reduce.6.cloned.1.call-update) | async-done | bytes 131088 | tf_op jit(solution)/shard_map/pmax | solution.py:56
  420.1 1.7 fusion.20
  421.7 11.3 bitcast_multiply_fusion
  433.1 565.2 %all-reduce.10.cloned.1.call-done = (f32[8,128,4096]{1,2,0:T(8,128)}, f32[8,128,32]{1,2,0:T(8,128)}) async-done(((f32[8,128,4096]{1,2,0:T(8,128)}, f32[8,128,32]{1,2,0:T(8,128)}), (f32[8,128,4096]{1,2,0:T(8,128)}, f32[8,128,32]{1,2,0:T(8,128)})) %all-reduce.10.cloned.1.call-update) | async-done | bytes 16908304 | tf_op jit(solution)/shard_map/psum | solution.py:69
  1000.6 2.1 fusion.9
  1002.8 216.5 %all-reduce.8.cloned.1.call-done = (f32[8,128,4096]{1,2,0:T(8,128)}, f32[8,128,32]{1,2,0:T(8,128)}) async-done(((f32[8,128,4096]{1,2,0:T(8,128)}, f32[8,128,32]{1,2,0:T(8,128)}), (f32[8,128,4096]{1,2,0:T(8,128)}, f32[8,128,32]{1,2,0:T(8,128)})) %all-reduce.8.cloned.1.call-update) | async-done | bytes 16908304 | tf_op jit(solution)/shard_map/psum | solution.py:69
  1220.5 5.3 constant_dynamic-slice_fusion.3
  1225.8 2.8 copy.49
  (96 shorter events, 59.2 us)
Async XLA Ops:
  6.5 991.8 %copy-start = (bf16[1024,1024]{1,0:T(8,128)(2,1)S(1)}, bf16[1024,1024]{1,0:T(8,128)(2,1)}, u32[]{:S(2)}) copy-start(bf16[1024,1024]{1,0:T(8,128)(2,1)} %param.12) | copy-start | bytes 6291460
  6.5 33.1 %all-gather.3.cloned.1.call-start = ((), (), s32[]{:S(2)}) async-start(), calls=%async_computation | async-start | bytes 1310720 | tf_op jit(solution)/shard_map/all_gather | solution.py:50
  8.5 86.7 %all-gather.5.cloned.1.call-start = ((), (), s32[]{:S(2)}) async-start(), calls=%async_computation.1 | async-start | bytes 9437184 | tf_op jit(solution)/shard_map/all_gather | solution.py:51
  39.7 380.4 %all-reduce.6.cloned.1.call-start = ((), (), s32[]{:S(2)}) async-start(), calls=%async_computation.2 | async-start | bytes 262144 | tf_op jit(solution)/shard_map/pmax | solution.py:56
  39.8 67.9 %copy-start.4 = (s32[8]{0:T(128)S(1)}, s32[8]{0:T(128)}, u32[]{:S(2)}) copy-start(s32[8]{0:T(128)} %param.14) | copy-start | bytes 100
  115.9 3.2 copy-start.1
  139.3 3.2 copy-start.1
  162.7 3.2 copy-start.1
  186.2 3.2 copy-start.1
  209.6 3.2 copy-start.1
  233.1 3.2 copy-start.1
  256.6 3.2 copy-start.1
  280.0 3.2 copy-start.1
  295.3 703.0 %all-reduce.10.cloned.1.call-start = ((), (), s32[]{:S(2)}) async-start(), calls=%async_computation.4 | async-start | bytes 33816576 | tf_op jit(solution)/shard_map/psum | solution.py:69
  433.0 786.3 %all-reduce.8.cloned.1.call-start = ((), (), s32[]{:S(2)}) async-start(), calls=%async_computation.3 | async-start | bytes 33816576 | tf_op jit(solution)/shard_map/psum | solution.py:69
  998.3 0.7 copy-start.3
  998.3 1.3 copy-start.2
Sparse Core Ops, SparseCore 0:
  8.9 30.6 all-gather.2
  41.5 53.6 all-gather.4
  295.4 124.6 all-reduce.5
  433.2 565.1 all-reduce.9
  1002.2 217.0 all-reduce.7
